TPU v7x, 256 devices: a 4x2x16 block of a 4x16x16 slice. The times are simulated.
256 devices in a mesh: grp: 2 (over y), blk: 16 (over z), node: 4 (over x), pair: 2 (over core).
Axes of the slice: x: 4, y: 2, z: 16, core: 2. Of those that a mesh axis runs over, the one named last changes fastest.
The devices are a block of a 4x16x16 slice.
Arguments:
- query: bfloat16 [18432, 1280], P(('grp', 'blk', 'node'), 'pair'), parts along dimension 0, may hold values from -600 to 600
- key: bfloat16 [18432, 1280], P(('grp', 'blk', 'node'), 'pair'), parts along dimension 0, may hold values from -25 to 25
- value: bfloat16 [18432, 1280], P(('grp', 'blk', 'node'), 'pair'), parts along dimension 0, may hold values from -6 to 6
- out_weight: bfloat16 [1280, 1280], P('pair'), may hold values from -0.15625 to 0.15625
Outputs:
- mixed: bfloat16 [18432, 1280], P(('grp', 'blk', 'node', 'pair')), parts along dimension 0
There are 2 independent parts, one for each index of `grp`. A program takes and returns all parts, laid end to end along the dimension named above; an argument that names none is the same for every part. Nothing has to cross between parts.
All inputs are finite; a program needn't handle non-finite values.
Results may differ from a plain program's by a relative error of at most 0.011.
Values may be sent and summed in bfloat16 or wider, within the bound.
A program may use at most 128 MiB of HBM per device.

v0:
```python
import math

import jax
import jax.numpy as jnp
from jax import lax
from jax.sharding import PartitionSpec as P

HD = 64


lowest = -1e30


def in_one_piece(arrays, axis, dim, along):
    both = jnp.concatenate(arrays, axis=along)
    filled, at, gathered = (lax.all_gather(both, axis, axis=dim, tiled=True), 0, [])
    for a in arrays:
        gathered.append(lax.slice_in_dim(filled, at, at + a.shape[along], axis=along))
        at += a.shape[along]
    return tuple(gathered)


def split_up(array, dim, length):
    lengths = array.shape
    tiles = array.reshape(*lengths[:dim], length, lengths[dim] // length, *lengths[dim + 1 :])
    return jnp.moveaxis(tiles, dim, 0)


def sent_and_summed(array, axis, dim):
    length = lax.axis_size(axis)
    tiles = lax.all_to_all(split_up(array, dim, length), axis, 0, 0, tiled=True)
    return jnp.sum(tiles.astype(jnp.float32), axis=0)


def block_rows(count):
    size = count
    while size > 1024 and size % 2 == 0:
        size = size // 2
    return size


def attend(carry, keys_piece, values_piece, queries):
    count = keys_piece.shape[0]
    size = block_rows(count)
    q_rows, heads, width = queries.shape
    scale = 1.0 / math.sqrt(width)

    def update(turn, state):
        peak, total, accum = state
        key_block = lax.dynamic_slice_in_dim(keys_piece, turn * size, size, 0).reshape(
            size, heads, width
        )
        value_block = lax.dynamic_slice_in_dim(values_piece, turn * size, size, 0).reshape(
            size, heads, width
        )
        scores = (
            jnp.einsum("qhd,khd->hqk", queries, key_block, preferred_element_type=jnp.float32)
            * scale
        )
        fresh = jnp.maximum(peak, jnp.max(scores, axis=2))
        expo = jnp.exp(scores - fresh[:, :, None])
        factor = jnp.exp(peak - fresh)
        total = total * factor + jnp.sum(expo, axis=2)
        weighted = jnp.einsum(
            "hqk,khd->qhd",
            expo.astype(jnp.bfloat16),
            value_block,
            preferred_element_type=jnp.float32,
        )
        accum = (accum.reshape(q_rows, heads, width) * factor.T[:, :, None] + weighted).reshape(
            q_rows, heads * width
        )
        return (fresh, total, accum)

    return lax.fori_loop(0, count // size, update, carry)


def start_state(heads, count, features):
    return (
        jnp.full((heads, count), lowest, jnp.float32),
        jnp.zeros((heads, count), jnp.float32),
        jnp.zeros((count, features), jnp.float32),
    )


def per_device(query, key, value, out_weight):
    rows, features = query.shape
    heads = features // HD
    gathered = lax.all_gather(query, "node", axis=0, tiled=True)
    count = gathered.shape[0]
    q_three = gathered.reshape(count, heads, HD)
    piece = in_one_piece((key, value), "blk", 0, 1)
    peak, total, accum = attend(start_state(heads, count, features), piece[0], piece[1], q_three)
    nodes = lax.axis_size("node")
    acc_parts = accum.reshape(nodes, rows, features)
    peak_parts = peak.T.reshape(nodes, rows, heads)
    total_parts = total.T.reshape(nodes, rows, heads)
    acc_in = lax.all_to_all(acc_parts, "node", split_axis=0, concat_axis=0, tiled=True)
    peak_in = lax.all_to_all(peak_parts, "node", split_axis=0, concat_axis=0, tiled=True)
    total_in = lax.all_to_all(total_parts, "node", split_axis=0, concat_axis=0, tiled=True)
    sources = acc_in.shape[0]
    items = acc_in.shape[1]
    best = jnp.max(peak_in, axis=0)
    weight = jnp.exp(peak_in - best[None])
    summed = jnp.sum(weight * total_in, axis=0)
    joined = jnp.sum(acc_in.reshape(sources, items, heads, HD) * weight[:, :, :, None], axis=0)
    attn = (joined / summed[:, :, None]).reshape(items, features).astype(jnp.bfloat16)
    mixed = sent_and_summed(
        jnp.dot(attn, out_weight, preferred_element_type=jnp.float32).astype(jnp.bfloat16),
        "pair",
        0,
    )
    return mixed.astype(jnp.bfloat16)


def solution(mesh):
    in_specs = (
        P(("grp", "blk", "node"), "pair"),
        P(("grp", "blk", "node"), "pair"),
        P(("grp", "blk", "node"), "pair"),
        P("pair", None),
    )
    out_specs = P(("grp", "blk", "node", "pair"), None)
    return jax.shard_map(
        per_device, mesh=mesh, in_specs=in_specs, out_specs=out_specs, check_vma=False
    )
```

profile of v0, /device:TPU:33, one launch (start us, length us, event | category | flops | bytes accessed | tf_op | source)
XLA Modules:
  0.0 282.9 jit_solution(13159151438150740473)
XLA Ops:
  8.5 12.0 %all_gather.7 = bf16[576,640]{1,0:T(8,128)(2,1)S(1)} all-gather(bf16[144,640]{1,0:T(8,128)(2,1)} %param.6), channel_id=1, replica_groups=mesh['grp'=2,'blk'=16,'node'=4,'pair'=2] {'node'}, dimensions={0}, use_global_device_ids=true | all-gather | bytes 921600 | tf_op jit(solution)/shard_map/all_gather | solution.py:89
  21.8 79.6 %all-gather.2.cloned.1.call-done = bf16[2304,1280]{1,0:T(8,128)(2,1)} async-done(((bf16[144,1280]{1,0:T(8,128)(2,1)}), bf16[2304,1280]{1,0:T(8,128)(2,1)}) %all-gather.2.cloned.1.call-update) | async-done | bytes 5898256 | tf_op jit(solution)/shard_map/all_gather | solution.py:16
  101.4 5.7 %fusion.12 = (bf16[2304,640]{1,0:T(8,128)(2,1)}, bf16[2304,640]{1,0:T(8,128)(2,1)}) fusion(bf16[2304,1280]{1,0:T(8,128)(2,1)} %all-gather.2.cloned.1.call-done), kind=kLoop, calls=%fused_computation.23 | loop fusion | bytes 11796480 | tf_op jit(solution)/shard_map/slice | solution.py:18
  108.4 120.4 %while.18 = (s32[]{:T(128)}, f32[10,576]{1,0:T(8,128)S(1)}, f32[10,576]{1,0:T(8,128)S(1)}, f32[576,640]{0,1:T(8,128)}, bf16[2304,640]{1,0:T(8,128)(2,1)}, /*inde...) while((s32[]{:T(128)}, f32[10,576]{1,0:T(8,128)S(1)}, ...), condition=%wide.region_3.0_spmd.clone, body=%wide.region_0.0_spmd.clone.sunk | while | flops 876660480 | bytes 51241136 | solution.py:75
  112.3 8.5 %bitcast_reduce_fusion.3 = (f32[10,576]{1,0:T(8,128)S(1)}, f32[10,576,576]{2,1,0:T(8,128)}) fusion(bf16[576,10,64]{0,2,1:T(8,128)(2,1)S(1)} %bitcast.70, bf16[576,10,64]{0,2,1:T(8,128)(2,1)} %get-tuple-element.278), kind=kOutput, calls=%fused_computation.1.clone.1 | convolution fusion | flops 431303040 | bytes 14768640 | tf_op jit(solution)/shard_map/while/body/eval_jaxpr/qhd,khd->hqk/dot_general | solution.py:57
  120.8 7.7 %fusion.29 = f32[10,576]{1,0:T(8,128)S(1)} fusion(f32[10,576,576]{2,1,0:T(8,128)} %get-tuple-element.248, f32[10,576]{1,0:T(8,128)S(1)} %get-tuple-element.274), kind=kLoop, calls=%fused_computation.4.clone.1 | loop fusion | flops 9947520 | bytes 13317120 | tf_op jit(solution)/shard_map/while/body/eval_jaxpr/reduce_sum | solution.py:63
  128.9 9.6 %bitcast_add_fusion.2 = f32[576,10,64]{0,2,1:T(8,128)} fusion(f32[576,10,64]{0,2,1:T(8,128)} %bitcast.72, bf16[576,10,64]{0,2,1:T(8,128)(2,1)S(1)} %bitcast.71, f32[10,576,576]{2,1,0:T(8,128)} %get-tuple-element.248, f32[10,576]{1,0:T(8,128)S(1)} %get-tuple-element.274, f32[576,10]{0,1:T(8,128)S(1)} %get-tuple-element.250), kind=kOutput, calls=%fused_computation.8.clone.1 | convolution fusion | flops 435363840 | bytes 17003520 | tf_op jit(solution)/shard_map/while/body/eval_jaxpr/hqk,khd->qhd/dot_general | solution.py:64
  142.3 8.5 %bitcast_reduce_fusion.3 = (f32[10,576]{1,0:T(8,128)S(1)}, f32[10,576,576]{2,1,0:T(8,128)}) fusion(bf16[576,10,64]{0,2,1:T(8,128)(2,1)S(1)} %bitcast.70, bf16[576,10,64]{0,2,1:T(8,128)(2,1)} %get-tuple-element.278), kind=kOutput, calls=%fused_computation.1.clone.1 | convolution fusion | flops 431303040 | bytes 14768640 | tf_op jit(solution)/shard_map/while/body/eval_jaxpr/qhd,khd->hqk/dot_general | solution.py:57
  150.8 7.7 %fusion.29 = f32[10,576]{1,0:T(8,128)S(1)} fusion(f32[10,576,576]{2,1,0:T(8,128)} %get-tuple-element.248, f32[10,576]{1,0:T(8,128)S(1)} %get-tuple-element.274), kind=kLoop, calls=%fused_computation.4.clone.1 | loop fusion | flops 9947520 | bytes 13317120 | tf_op jit(solution)/shard_map/while/body/eval_jaxpr/reduce_sum | solution.py:63
  159.0 9.6 %bitcast_add_fusion.2 = f32[576,10,64]{0,2,1:T(8,128)} fusion(f32[576,10,64]{0,2,1:T(8,128)} %bitcast.72, bf16[576,10,64]{0,2,1:T(8,128)(2,1)S(1)} %bitcast.71, f32[10,576,576]{2,1,0:T(8,128)} %get-tuple-element.248, f32[10,576]{1,0:T(8,128)S(1)} %get-tuple-element.274, f32[576,10]{0,1:T(8,128)S(1)} %get-tuple-element.250), kind=kOutput, calls=%fused_computation.8.clone.1 | convolution fusion | flops 435363840 | bytes 17003520 | tf_op jit(solution)/shard_map/while/body/eval_jaxpr/hqk,khd->qhd/dot_general | solution.py:64
  172.4 8.5 %bitcast_reduce_fusion.3 = (f32[10,576]{1,0:T(8,128)S(1)}, f32[10,576,576]{2,1,0:T(8,128)}) fusion(bf16[576,10,64]{0,2,1:T(8,128)(2,1)S(1)} %bitcast.70, bf16[576,10,64]{0,2,1:T(8,128)(2,1)} %get-tuple-element.278), kind=kOutput, calls=%fused_computation.1.clone.1 | convolution fusion | flops 431303040 | bytes 14768640 | tf_op jit(solution)/shard_map/while/body/eval_jaxpr/qhd,khd->hqk/dot_general | solution.py:57
  180.9 7.7 %fusion.29 = f32[10,576]{1,0:T(8,128)S(1)} fusion(f32[10,576,576]{2,1,0:T(8,128)} %get-tuple-element.248, f32[10,576]{1,0:T(8,128)S(1)} %get-tuple-element.274), kind=kLoop, calls=%fused_computation.4.clone.1 | loop fusion | flops 9947520 | bytes 13317120 | tf_op jit(solution)/shard_map/while/body/eval_jaxpr/reduce_sum | solution.py:63
  189.1 9.6 %bitcast_add_fusion.2 = f32[576,10,64]{0,2,1:T(8,128)} fusion(f32[576,10,64]{0,2,1:T(8,128)} %bitcast.72, bf16[576,10,64]{0,2,1:T(8,128)(2,1)S(1)} %bitcast.71, f32[10,576,576]{2,1,0:T(8,128)} %get-tuple-element.248, f32[10,576]{1,0:T(8,128)S(1)} %get-tuple-element.274, f32[576,10]{0,1:T(8,128)S(1)} %get-tuple-element.250), kind=kOutput, calls=%fused_computation.8.clone.1 | convolution fusion | flops 435363840 | bytes 17003520 | tf_op jit(solution)/shard_map/while/body/eval_jaxpr/hqk,khd->qhd/dot_general | solution.py:64
  202.5 8.5 %bitcast_reduce_fusion.3 = (f32[10,576]{1,0:T(8,128)S(1)}, f32[10,576,576]{2,1,0:T(8,128)}) fusion(bf16[576,10,64]{0,2,1:T(8,128)(2,1)S(1)} %bitcast.70, bf16[576,10,64]{0,2,1:T(8,128)(2,1)} %get-tuple-element.278), kind=kOutput, calls=%fused_computation.1.clone.1 | convolution fusion | flops 431303040 | bytes 14768640 | tf_op jit(solution)/shard_map/while/body/eval_jaxpr/qhd,khd->hqk/dot_general | solution.py:57
  211.0 7.7 %fusion.29 = f32[10,576]{1,0:T(8,128)S(1)} fusion(f32[10,576,576]{2,1,0:T(8,128)} %get-tuple-element.248, f32[10,576]{1,0:T(8,128)S(1)} %get-tuple-element.274), kind=kLoop, calls=%fused_computation.4.clone.1 | loop fusion | flops 9947520 | bytes 13317120 | tf_op jit(solution)/shard_map/while/body/eval_jaxpr/reduce_sum | solution.py:63
  219.2 9.6 %bitcast_add_fusion.2 = f32[576,10,64]{0,2,1:T(8,128)} fusion(f32[576,10,64]{0,2,1:T(8,128)} %bitcast.72, bf16[576,10,64]{0,2,1:T(8,128)(2,1)S(1)} %bitcast.71, f32[10,576,576]{2,1,0:T(8,128)} %get-tuple-element.248, f32[10,576]{1,0:T(8,128)S(1)} %get-tuple-element.274, f32[576,10]{0,1:T(8,128)S(1)} %get-tuple-element.250), kind=kOutput, calls=%fused_computation.8.clone.1 | convolution fusion | flops 435363840 | bytes 17003520 | tf_op jit(solution)/shard_map/while/body/eval_jaxpr/hqk,khd->qhd/dot_general | solution.py:64
  229.6 4.0 %all-to-all-start.1 = ((f32[4,1,1440]{2,1,0:T(1,128)}), f32[4,1,1440]{2,1,0:T(1,128)S(1)}, u32[]{:S(2)}, u32[]{:S(2)}) async-start(f32[4,1,1440]{2,1,0:T(1,128)} %reshape.64), calls=%async_computation.1 | async-start | bytes 49152 | tf_op jit(solution)/shard_map/all_to_all | solution.py:99
  234.4 3.4 %all-to-all-done.1 = f32[4,1,1440]{2,1,0:T(1,128)S(1)} async-done(((f32[4,1,1440]{2,1,0:T(1,128)}), f32[4,1,1440]{2,1,0:T(1,128)S(1)}, u32[]{:S(2)}, u32[]{:S(2)}) %all-to-all-start.1) | async-done | bytes 23072 | tf_op jit(solution)/shard_map/all_to_all | solution.py:99
  237.9 3.3 %all-to-all-start.2 = ((f32[4,1,1440]{2,1,0:T(1,128)}), f32[4,1,1440]{2,1,0:T(1,128)S(1)}, u32[]{:S(2)}, u32[]{:S(2)}) async-start(f32[4,1,1440]{2,1,0:T(1,128)} %reshape.66), calls=%async_computation.2 | async-start | bytes 49152 | tf_op jit(solution)/shard_map/all_to_all | solution.py:100
  241.2 3.0 %copy.33 = f32[576,640]{1,0:T(8,128)} copy(f32[576,640]{0,1:T(8,128)} %get-tuple-element.131) | data formatting | bytes 2949120 | tf_op jit(solution)/shard_map/while | solution.py:75
  245.4 3.6 %all-to-all-start = ((f32[4,144,640]{2,1,0:T(8,128)}), f32[4,144,640]{2,1,0:T(8,128)S(1)}, u32[]{:S(2)}, u32[]{:S(2)}) async-start(f32[4,144,640]{2,1,0:T(8,128)} %bitcast.1), calls=%async_computation | async-start | bytes 2949120 | tf_op jit(solution)/shard_map/all_to_all | solution.py:98
  252.9 3.0 %copy.35 = f32[4,144,640]{2,1,0:T(8,128)} copy(f32[4,144,640]{1,2,0:T(8,128)} %bitcast.75) | data formatting | bytes 2949120 | tf_op jit(solution)/shard_map/mul | solution.py:106
  258.1 3.0 %all-to-all-done = f32[4,144,640]{2,1,0:T(8,128)S(1)} async-done(((f32[4,144,640]{2,1,0:T(8,128)}), f32[4,144,640]{2,1,0:T(8,128)S(1)}, u32[]{:S(2)}, u32[]{:S(2)}) %all-to-all-start) | async-done | bytes 1474592 | tf_op jit(solution)/shard_map/all_to_all | solution.py:98
  263.1 12.2 %all_to_all.20 = bf16[2,72,1280]{2,1,0:T(8,128)(2,1)S(1)} all-to-all(bf16[2,72,1280]{2,1,0:T(8,128)(2,1)S(1)} %bitcast.79), channel_id=1, replica_groups=mesh['grp'=2,'blk'=16,'node'=4,'pair'=2] {'pair'}, dimensions={0} | all-to-all | bytes 737280 | tf_op jit(solution)/shard_map/all_to_all | solution.py:31
  (53 shorter events, 33.1 us)
Async XLA Ops:
  6.5 256.1 %copy-start = (bf16[640,1280]{1,0:T(8,128)(2,1)S(1)}, bf16[640,1280]{1,0:T(8,128)(2,1)}, u32[]{:S(2)}) copy-start(bf16[640,1280]{1,0:T(8,128)(2,1)} %param.9) | copy-start | bytes 4915204
  6.6 94.9 %all-gather.2.cloned.1.call-start = ((), (), s32[]{:S(2)}) async-start(), calls=%async_computation.4 | async-start | bytes 6266880 | tf_op jit(solution)/shard_map/all_gather | solution.py:16
  229.6 8.2 %all-to-all-start.1 = ((f32[4,1,1440]{2,1,0:T(1,128)}), f32[4,1,1440]{2,1,0:T(1,128)S(1)}, u32[]{:S(2)}, u32[]{:S(2)}) async-start(f32[4,1,1440]{2,1,0:T(1,128)} %reshape.64), calls=%async_computation.1 | async-start | bytes 49152 | tf_op jit(solution)/shard_map/all_to_all | solution.py:99
  237.9 7.5 %all-to-all-start.2 = ((f32[4,1,1440]{2,1,0:T(1,128)}), f32[4,1,1440]{2,1,0:T(1,128)S(1)}, u32[]{:S(2)}, u32[]{:S(2)}) async-start(f32[4,1,1440]{2,1,0:T(1,128)} %reshape.66), calls=%async_computation.2 | async-start | bytes 49152 | tf_op jit(solution)/shard_map/all_to_all | solution.py:100
  245.4 15.7 %all-to-all-start = ((f32[4,144,640]{2,1,0:T(8,128)}), f32[4,144,640]{2,1,0:T(8,128)S(1)}, u32[]{:S(2)}, u32[]{:S(2)}) async-start(f32[4,144,640]{2,1,0:T(8,128)} %bitcast.1), calls=%async_computation | async-start | bytes 2949120 | tf_op jit(solution)/shard_map/all_to_all | solution.py:98
Sparse Core Ops, SparseCore 0:
  9.1 92.2 all-gather.1
where the time goes:
time: 284 us; the launch traced here: 283 us
  waiting for transfers between devices  87.2 us (31%)
  matrix products  72.9 us (26%)
  local copies, waits for them, and re-layouts  37.3 us (13%)
  other arithmetic  36.7 us (13%)
  blocking collectives  24.2 us (9%)
  between operations  13.5 us (5%)
  starting transfers between devices  11 us (4%)
    all_gather x1, waiting for transfers between devices, in_one_piece(): lax.all_gather(both, axis, axis=dim, tiled=True)  79.6 us
    dot_general x4, matrix products, update(): jnp.einsum('hqk,khd->qhd', expo.astype(jnp.bfloat16), value_block, prefer...  38.5 us
    dot_general x4, matrix products, update(): jnp.einsum('qhd,khd->hqk', queries, key_block, preferred_element_type=jnp...  33.9 us
    reduce_sum x4, other arithmetic, update(): total = total * factor + jnp.sum(expo, axis=2)  30.9 us
    all_to_all x1, blocking collectives, sent_and_summed(): tiles = lax.all_to_all(split_up(array, dim, length), axis, 0, 0, tiled=True)  12.2 us
    all_gather x1, blocking collectives, per_device(): gathered = lax.all_gather(query, 'node', axis=0, tiled=True)  12 us
    dynamic_slice x8, local copies, waits for them, and re-layouts, update(): lax.dynamic_slice_in_dim(values_piece, turn * size, size, 0)  10.9 us
    dynamic_slice x4, local copies, waits for them, and re-layouts, update(): lax.dynamic_slice_in_dim(keys_piece, turn * size, size, 0)  5.95 us
  transfers between devices with their start and end apart: 4, of which 4 were waited for; matrix products, arithmetic and copies ran while one was open for 5% of the time, Pallas kernels for 0%

commit v1 on v0

v1 whole, which is shorter than its diff:
```python
import functools
import math

import jax
import jax.numpy as jnp
from jax import lax
from jax.experimental import pallas as pl
from jax.experimental.pallas import tpu as pltpu
from jax.sharding import PartitionSpec as P

HD = 64
LANES = 128
MESH = pl.DeviceIdType.MESH


def kernel(
    nz, nx, q_hbm, k_hbm, v_hbm, w_hbm, out_ref,
    kv, qall, qs, w, ml, acc, st_in, cb, cin, pacc, sbuf, rbuf,
    kv_send, kv_recv, q_send, q_recv, st_send, st_recv, c_send, c_recv, p_send, p_recv, loc,
):
    rows, features = q_hbm.shape
    pairs = features // LANES
    half = nz // 2
    nq = nx * rows
    z = lax.axis_index("blk")
    x = lax.axis_index("node")
    p = lax.axis_index("pair")
    z_next = (lax.rem(z + 1, nz), lax.rem(z + nz - 1, nz))
    scale2 = (1.0 / math.sqrt(HD)) * math.log2(math.e)

    def node(j):
        return lax.rem(x + j, nx)

    barrier = pltpu.get_barrier_semaphore()
    for d in range(2):
        pl.semaphore_signal(barrier, inc=1, device_id={"blk": z_next[d]}, device_id_type=MESH)
    for j in range(1, nx):
        pl.semaphore_signal(barrier, inc=1, device_id={"node": node(j)}, device_id_type=MESH)
    pl.semaphore_signal(barrier, inc=1, device_id={"pair": 1 - p}, device_id_type=MESH)

    def own_copy(r, part):
        src = (k_hbm, v_hbm)[part]
        return pltpu.make_async_copy(
            src.at[:, pl.ds(r * LANES, LANES)], kv.at[half, r, 0, part], loc.at[r, part]
        )

    for r in range(pairs):
        for part in range(2):
            own_copy(r, part).start()
    q_copy = pltpu.make_async_copy(q_hbm, qall.at[x], loc.at[pairs, 0])
    q_copy.start()
    w_copy = pltpu.make_async_copy(w_hbm, w, loc.at[pairs, 1])
    w_copy.start()
    pl.semaphore_wait(barrier, nx + 2)

    def full_msg(src, s, r, d):
        return pltpu.make_async_remote_copy(
            src_ref=src, dst_ref=kv.at[s, r, d],
            send_sem=kv_send.at[s - 1, r, d], recv_sem=kv_recv.at[s - 1, r, d],
            device_id={"blk": z_next[d]}, device_id_type=MESH,
        )

    def last_msg(src, r, d):
        return pltpu.make_async_remote_copy(
            src_ref=src, dst_ref=kv.at[half, r, 1, d],
            send_sem=kv_send.at[half - 1, r, d], recv_sem=kv_recv.at[half - 1, r, d],
            device_id={"blk": z_next[d]}, device_id_type=MESH,
        )

    def q_msg(j):
        return pltpu.make_async_remote_copy(
            src_ref=qall.at[x], dst_ref=qall.at[x],
            send_sem=q_send.at[j - 1], recv_sem=q_recv.at[j - 1],
            device_id={"node": node(j)}, device_id_type=MESH,
        )

    def q_arrival(j):
        return pltpu.make_async_remote_copy(
            src_ref=qall.at[node(nx - j)], dst_ref=qall.at[node(nx - j)],
            send_sem=q_send.at[j - 1], recv_sem=q_recv.at[j - 1],
            device_id={"node": node(j)}, device_id_type=MESH,
        )

    for r in range(pairs):
        own_copy(r, 0).wait()
        own_copy(r, 1).wait()
        for d in range(2):
            full_msg(kv.at[half, r, 0], 1, r, d).start()
    q_copy.wait()
    for j in range(1, nx):
        q_msg(j).start()

    ml[:, 0:1, :] = jnp.full((pairs, 1, 2 * nq), -1e30, jnp.float32)
    ml[:, 1:2, :] = jnp.zeros((pairs, 1, 2 * nq), jnp.float32)
    acc[...] = jnp.zeros(acc.shape, jnp.float32)

    def forward(t):
        s = t // pairs + 1
        r = lax.rem(t, pairs)
        for d in range(2):
            @pl.when(s < half)
            def _():
                full_msg(kv.at[half, r, 0], s, r, d).wait_recv()

            @pl.when(s == half)
            def _():
                last_msg(kv.at[half, r, 0, d], r, d).wait_recv()

            @pl.when(s < half - 1)
            def _():
                full_msg(kv.at[s, r, d], s + 1, r, d).start()

            @pl.when(s == half - 1)
            def _():
                last_msg(kv.at[s, r, d, d], r, d).start()

    width = 256

    def compute(t):
        s = t // pairs + 1
        r = lax.rem(t, pairs)
        keys = kv[s, r, :, 0].reshape(2 * rows, LANES)
        values = kv[s, r, :, 1].reshape(2 * rows, LANES)
        for lo in range(0, 2 * nq, width):
            hi = min(lo + width, 2 * nq)
            sc = lax.dot_general(
                keys, qs[r, lo:hi, :], (((1,), (1,)), ((), ())),
                preferred_element_type=jnp.float32,
            )
            old = ml[r, 0:1, lo:hi]
            new = jnp.maximum(old, jnp.max(sc, axis=0, keepdims=True))
            expo = jnp.exp2((sc - new) * scale2)
            factor = jnp.exp2((old - new) * scale2)
            ml[r, 0:1, lo:hi] = new
            ml[r, 1:2, lo:hi] = ml[r, 1:2, lo:hi] * factor + jnp.sum(expo, axis=0, keepdims=True)
            weighted = lax.dot_general(
                values, expo.astype(jnp.bfloat16), (((0,), (0,)), ((), ())),
                preferred_element_type=jnp.float32,
            )
            acc[r, :, lo:hi] = acc[r, :, lo:hi] * factor + weighted

    total = half * pairs

    @pl.loop(0, pairs)
    def _(t):
        forward(t)

    for j in range(1, nx):
        q_arrival(j).wait_recv()
    lane = lax.broadcasted_iota(jnp.int32, (rows, LANES), 1)
    for xa in range(nx):
        for r in range(pairs):
            block = qall[xa, :, r * LANES:(r + 1) * LANES].astype(jnp.float32)
            qs[r, xa * rows:(xa + 1) * rows, :] = jnp.where(lane < HD, block, 0.0).astype(jnp.bfloat16)
            qs[r, nq + xa * rows:nq + (xa + 1) * rows, :] = jnp.where(
                lane < HD, 0.0, block
            ).astype(jnp.bfloat16)

    def done_by(t):
        return jnp.where(t < pairs, 0, jnp.where(t < 2 * pairs - 1, t + 1 - pairs, t + 1))

    def st_msg(r, j):
        return pltpu.make_async_remote_copy(
            src_ref=ml.at[r], dst_ref=st_in.at[r, j - 1],
            send_sem=st_send.at[r, j - 1], recv_sem=st_recv.at[r, j - 1],
            device_id={"node": node(j)}, device_id_type=MESH,
        )

    def c_msg(r, j):
        return pltpu.make_async_remote_copy(
            src_ref=cb.at[r, node(j)], dst_ref=cin.at[r, j - 1],
            send_sem=c_send.at[r, j - 1], recv_sem=c_recv.at[r, j - 1],
            device_id={"node": node(j)}, device_id_type=MESH,
        )

    def spread(r):
        for j in range(1, nx):
            st_msg(r, j).wait_recv()
        best = ml[r, 0:1, :]
        for j in range(1, nx):
            best = jnp.maximum(best, st_in[r, j - 1, 0:1, :])
        mine = jnp.exp2((ml[r, 0:1, :] - best) * scale2)
        summed = ml[r, 1:2, :] * mine
        for j in range(1, nx):
            summed += st_in[r, j - 1, 1:2, :] * jnp.exp2((st_in[r, j - 1, 0:1, :] - best) * scale2)
        turned = (acc[r] * (mine / summed)).T
        lanes = lax.broadcasted_iota(jnp.int32, (nq, LANES), 1)
        both = jnp.where(lanes < HD, turned[:nq], turned[nq:]).astype(jnp.bfloat16)
        for xa in range(nx):
            cb[r, xa] = both[xa * rows:(xa + 1) * rows]
        for j in range(1, nx):
            c_msg(r, j).start()

    def project(r):
        for j in range(1, nx):
            c_msg(r, j).wait_recv()
        attn = cb[r, x].astype(jnp.float32)
        for j in range(1, nx):
            attn += cin[r, j - 1].astype(jnp.float32)
        pacc[...] += jnp.dot(
            attn.astype(jnp.bfloat16), w[pl.ds(r * LANES, LANES), :],
            preferred_element_type=jnp.float32,
        )

    @pl.loop(pairs, total)
    def _(t):
        forward(t)

        @pl.loop(done_by(t - 1), done_by(t))
        def _(c):
            compute(c)

        @pl.when(t >= total - pairs)
        def _():
            r = t - (total - pairs)
            for j in range(1, nx):
                st_msg(r, j).start()

    w_copy.wait()
    pacc[...] = jnp.zeros(pacc.shape, jnp.float32)

    @pl.loop(0, pairs)
    def _(r):
        spread(r)

    @pl.loop(0, pairs)
    def _(r):
        project(r)

    mine_rows = rows // 2
    sbuf[...] = pacc[pl.ds(pl.multiple_of((1 - p) * mine_rows, 8), mine_rows), :].astype(jnp.bfloat16)
    swap = pltpu.make_async_remote_copy(
        src_ref=sbuf, dst_ref=rbuf, send_sem=p_send, recv_sem=p_recv,
        device_id={"pair": 1 - p}, device_id_type=MESH,
    )
    swap.start()
    swap.wait_recv()
    out_ref[...] = (
        pacc[pl.ds(pl.multiple_of(p * mine_rows, 8), mine_rows), :] + rbuf[...].astype(jnp.float32)
    ).astype(out_ref.dtype)

    swap.wait_send()
    for j in range(1, nx):
        q_msg(j).wait_send()

    @pl.loop(0, pairs)
    def _(r):
        for j in range(1, nx):
            st_msg(r, j).wait_send()
            c_msg(r, j).wait_send()
        for d in range(2):
            last_msg(kv.at[half - 1, r, d, d], r, d).wait_send()

    @pl.loop(0, (half - 1) * pairs)
    def _(t):
        s = t // pairs + 1
        r = lax.rem(t, pairs)
        for d in range(2):
            full_msg(kv.at[half, r, 0], s, r, d).wait_send()


def solution(mesh):
    nz, nx = mesh.shape["blk"], mesh.shape["node"]
    half = nz // 2

    def per_device(query, key, value, out_weight):
        rows, features = query.shape
        pairs = features // LANES
        out_features = out_weight.shape[1]
        nq = nx * rows
        dma = pltpu.SemaphoreType.DMA
        any_space = pl.BlockSpec(memory_space=pl.ANY)
        bf16, f32 = jnp.bfloat16, jnp.float32
        return pl.pallas_call(
            functools.partial(kernel, nz, nx),
            out_shape=jax.ShapeDtypeStruct((rows // 2, out_features), bf16),
            in_specs=[any_space] * 4,
            out_specs=pl.BlockSpec(memory_space=pltpu.VMEM),
            scratch_shapes=[
                pltpu.VMEM((half + 1, pairs, 2, 2, rows, LANES), bf16),
                pltpu.VMEM((nx, rows, features), bf16),
                pltpu.VMEM((pairs, 2 * nq, LANES), bf16),
                pltpu.VMEM((features, out_features), bf16),
                pltpu.VMEM((pairs, 2, 2 * nq), f32),
                pltpu.VMEM((pairs, LANES, 2 * nq), f32),
                pltpu.VMEM((pairs, nx - 1, 2, 2 * nq), f32),
                pltpu.VMEM((pairs, nx, rows, LANES), bf16),
                pltpu.VMEM((pairs, nx - 1, rows, LANES), bf16),
                pltpu.VMEM((rows, out_features), f32),
                pltpu.VMEM((rows // 2, out_features), bf16),
                pltpu.VMEM((rows // 2, out_features), bf16),
                dma((half, pairs, 2)), dma((half, pairs, 2)),
                dma((nx - 1,)), dma((nx - 1,)),
                dma((pairs, nx - 1)), dma((pairs, nx - 1)),
                dma((pairs, nx - 1)), dma((pairs, nx - 1)),
                dma, dma, dma((pairs + 1, 2)),
            ],
            compiler_params=pltpu.CompilerParams(
                collective_id=0, has_side_effects=True, vmem_limit_bytes=48 * 1024 * 1024
            ),
        )(query, key, value, out_weight)

    tokens = P(("grp", "blk", "node"), "pair")
    return jax.shard_map(
        per_device,
        mesh=mesh,
        in_specs=(tokens, tokens, tokens, P("pair", None)),
        out_specs=P(("grp", "blk", "node", "pair"), None),
        check_vma=False,
    )
```

time: 284 us -> 126 us (0.44)
  Pallas kernels: 0 us -> 121 us
  waiting for transfers between devices: 87.2 us -> 0 us
  matrix products: 72.9 us -> 0 us
  other arithmetic: 36.7 us -> 0 us
  local copies, waits for them, and re-layouts: 37.3 us -> 4.87 us
  blocking collectives: 24.2 us -> 0 us
  between operations: 13.5 us -> 0.01 us
  starting transfers between devices: 11 us -> 0 us
    pallas_call x0 -> x1, Pallas kernels: none -> 121 us  [per_device(): pl.pallas_call(functools.partial(kernel, nz, nx), out_shape=jax.ShapeDtyp...]
    all_gather x1 -> x0, waiting for transfers between devices: 79.6 us -> none  [in_one_piece(): lax.all_gather(both, axis, axis=dim, tiled=True)]
    dot_general x9 -> x0, matrix products: 72.9 us -> none  [the longest x4 38.5 us: update(): jnp.einsum('hqk,khd->qhd', expo.astype(jnp.bfloat16), value_block, prefer...]
    reduce_sum x7 -> x0, other arithmetic: 33.2 us -> none  [the longest x4 30.9 us: update(): total = total * factor + jnp.sum(expo, axis=2)]
    dynamic_slice x12 -> x0, local copies, waits for them, and re-layouts: 16.8 us -> none  [the longest x8 10.9 us: update(): lax.dynamic_slice_in_dim(values_piece, turn * size, size, 0)]
    all_to_all x1 -> x0, blocking collectives: 12.2 us -> none  [sent_and_summed(): tiles = lax.all_to_all(split_up(array, dim, length), axis, 0, 0, tiled=True)]
    all_gather x1 -> x0, blocking collectives: 12 us -> none  [per_device(): gathered = lax.all_gather(query, 'node', axis=0, tiled=True)]
    all_to_all x3 -> x0, starting transfers between devices: 11 us -> none  [the longest x1 3.99 us: per_device(): lax.all_to_all(peak_parts, 'node', split_axis=0, concat_axis=0, tiled=True)]
  transfers between devices with their start and end apart: 4 -> 0, of which waited for: 4 -> 0; matrix products, arithmetic and copies ran while one was open for 5% -> 0% of each run, Pallas kernels for 0% -> 0%
where the time goes in v1:
time: 126 us
  Pallas kernels  121 us (96%)
  local copies, waits for them, and re-layouts  4.87 us (4%)
    pallas_call x1, Pallas kernels, per_device(): pl.pallas_call(functools.partial(kernel, nz, nx), out_shape=jax.ShapeDtyp...  121 us
    unnamed x9, local copies, waits for them, and re-layouts  4.87 us

profile of v1, /device:TPU:33, one launch (start us, length us, event | category | flops | bytes accessed | tf_op | source)
XLA Modules:
  0.0 125.9 jit_solution(495138693969995402)
XLA Ops:
  0.0 0.0 copy-start
  0.0 1.4 %copy-done = bf16[640,1280]{1,0:T(8,128)(2,1)S(1)} copy-done((bf16[640,1280]{1,0:T(8,128)(2,1)S(1)}, bf16[640,1280]{1,0:T(8,128)(2,1)}, u32[]{:S(2)}) %copy-start) | copy-done | bytes 1638424
  1.4 0.0 copy-start.1
  1.4 0.9 copy-done.1
  2.4 0.0 copy-start.2
  2.4 0.9 copy-done.2
  3.3 0.0 copy-start.3
  3.3 0.9 copy-done.3
  4.2 121.0 %shard_map.46 = bf16[72,1280]{1,0:T(8,128)(2,1)S(1)} custom-call(bf16[144,640]{1,0:T(8,128)(2,1)S(1)} %copy-done.1, bf16[144,640]{1,0:T(8,128)(2,1)S(1)} %copy-done.2, bf16[144,640]{1,0:T(8,128)(2,1)S(1)} %copy-done.3, bf16[640,1280]{1,0:T(8,128)(2,1)S(1)} %copy-done), custom_call_target="tpu_custom_call" | custom-call | tf_op jit(solution)/shard_map/pallas_call | solution.py:274
  125.2 0.7 copy.6
Async XLA Ops:
  0.0 1.4 %copy-start = (bf16[640,1280]{1,0:T(8,128)(2,1)S(1)}, bf16[640,1280]{1,0:T(8,128)(2,1)}, u32[]{:S(2)}) copy-start(bf16[640,1280]{1,0:T(8,128)(2,1)} %w_hbm.1) | copy-start | bytes 4915204
  1.4 0.9 copy-start.1
  2.4 0.9 copy-start.2
  3.3 0.9 copy-start.3

commit v2 on v1

--- a/solution.py
+++ b/solution.py
@@ -15,7 +15,7 @@
 
 def kernel(
     nz, nx, q_hbm, k_hbm, v_hbm, w_hbm, out_ref,
-    kv, qall, qs, w, ml, acc, st_in, cb, cin, pacc, sbuf, rbuf,
+    kv, qall, qs, w, ml, acc, st_in, cb, cin, pacc, turned_w, sbuf, rbuf,
     kv_send, kv_recv, q_send, q_recv, st_send, st_recv, c_send, c_recv, p_send, p_recv, loc,
 ):
     rows, features = q_hbm.shape
@@ -94,9 +94,19 @@
     ml[:, 1:2, :] = jnp.zeros((pairs, 1, 2 * nq), jnp.float32)
     acc[...] = jnp.zeros(acc.shape, jnp.float32)
 
+    fast = 2
+    slow = pairs - fast
+    turn = fast + 1
+
+    def unit(t):
+        ahead = (t < turn * half) & (lax.rem(t, turn) < fast)
+        k = jnp.where(t < turn * half, t // turn, t - fast * half)
+        s = jnp.where(ahead, t // turn, k // slow) + 1
+        r = jnp.where(ahead, lax.rem(t, turn), fast + lax.rem(k, slow))
+        return s, r
+
     def forward(t):
-        s = t // pairs + 1
-        r = lax.rem(t, pairs)
+        s, r = unit(t)
         for d in range(2):
             @pl.when(s < half)
             def _():
@@ -117,31 +127,48 @@
     width = 256
 
     def compute(t):
-        s = t // pairs + 1
-        r = lax.rem(t, pairs)
+        s, r = unit(t)
         keys = kv[s, r, :, 0].reshape(2 * rows, LANES)
-        values = kv[s, r, :, 1].reshape(2 * rows, LANES)
-        for lo in range(0, 2 * nq, width):
-            hi = min(lo + width, 2 * nq)
+        values = kv[s, r, :, 1].reshape(2 * rows, LANES).T
+        spans = [(lo, min(lo + width, 2 * nq)) for lo in range(0, 2 * nq, width)]
+
+        def scored(span):
+            lo, hi = span
             sc = lax.dot_general(
                 keys, qs[r, lo:hi, :], (((1,), (1,)), ((), ())),
                 preferred_element_type=jnp.float32,
             )
             old = ml[r, 0:1, lo:hi]
-            new = jnp.maximum(old, jnp.max(sc, axis=0, keepdims=True))
+            return sc, old, jnp.maximum(old, jnp.max(sc, axis=0, keepdims=True))
+
+        def weigh(span, sc, old, new):
+            lo, hi = span
             expo = jnp.exp2((sc - new) * scale2)
             factor = jnp.exp2((old - new) * scale2)
+            total_new = ml[r, 1:2, lo:hi] * factor + jnp.sum(expo, axis=0, keepdims=True)
+            top = HD if lo >= nq else 0
+            end = HD if hi <= nq else LANES
+            weighted = jnp.dot(
+                values[top:end], expo.astype(jnp.bfloat16), preferred_element_type=jnp.float32
+            )
+            return new, total_new, factor, weighted, top, end
+
+        ready = scored(spans[0])
+        results = []
+        for i, span in enumerate(spans):
+            following = scored(spans[i + 1]) if i + 1 < len(spans) else None
+            results.append(weigh(span, *ready))
+            ready = following
+        for (lo, hi), (new, total_new, factor, weighted, top, end) in zip(spans, results):
             ml[r, 0:1, lo:hi] = new
-            ml[r, 1:2, lo:hi] = ml[r, 1:2, lo:hi] * factor + jnp.sum(expo, axis=0, keepdims=True)
-            weighted = lax.dot_general(
-                values, expo.astype(jnp.bfloat16), (((0,), (0,)), ((), ())),
-                preferred_element_type=jnp.float32,
-            )
-            acc[r, :, lo:hi] = acc[r, :, lo:hi] * factor + weighted
+            ml[r, 1:2, lo:hi] = total_new
+            acc[r, top:end, lo:hi] = acc[r, top:end, lo:hi] * factor + weighted
 
     total = half * pairs
 
-    @pl.loop(0, pairs)
+    before_q = min(6, (turn * (half - 1) + 1) // 2)
+
+    @pl.loop(0, before_q)
     def _(t):
         forward(t)
 
@@ -157,7 +184,7 @@
             ).astype(jnp.bfloat16)
 
     def done_by(t):
-        return jnp.where(t < pairs, 0, jnp.where(t < 2 * pairs - 1, t + 1 - pairs, t + 1))
+        return jnp.clip(2 * (t - before_q + 1), 0, t + 1)
 
     def st_msg(r, j):
         return pltpu.make_async_remote_copy(
@@ -175,15 +202,8 @@
 
     def spread(r):
         for j in range(1, nx):
-            st_msg(r, j).wait_recv()
-        best = ml[r, 0:1, :]
-        for j in range(1, nx):
-            best = jnp.maximum(best, st_in[r, j - 1, 0:1, :])
-        mine = jnp.exp2((ml[r, 0:1, :] - best) * scale2)
-        summed = ml[r, 1:2, :] * mine
-        for j in range(1, nx):
-            summed += st_in[r, j - 1, 1:2, :] * jnp.exp2((st_in[r, j - 1, 0:1, :] - best) * scale2)
-        turned = (acc[r] * (mine / summed)).T
+            st_msg(r, j).start()
+        turned = (acc[r] * (1.0 / ml[r, 1:2, :])).T
         lanes = lax.broadcasted_iota(jnp.int32, (nq, LANES), 1)
         both = jnp.where(lanes < HD, turned[:nq], turned[nq:]).astype(jnp.bfloat16)
         for xa in range(nx):
@@ -193,16 +213,28 @@
 
     def project(r):
         for j in range(1, nx):
-            c_msg(r, j).wait_recv()
-        attn = cb[r, x].astype(jnp.float32)
-        for j in range(1, nx):
-            attn += cin[r, j - 1].astype(jnp.float32)
+            st_msg(r, j).wait_recv()
+        stats = [ml.at[r]] + [st_in.at[r, j - 1] for j in range(1, nx)]
+        best = functools.reduce(jnp.maximum, [st[0:1, :] for st in stats])
+        shares = [jnp.exp2((st[0:1, :] - best) * scale2) * st[1:2, :] for st in stats]
+        inverse = 1.0 / sum(shares)
+        blank = jnp.zeros((LANES - nx, 2 * nq), jnp.float32)
+        turned_w[...] = jnp.concatenate([share * inverse for share in shares] + [blank], axis=0).T
+        mine_a = turned_w[pl.ds(pl.multiple_of(x * rows, 8), rows), :]
+        mine_b = turned_w[pl.ds(pl.multiple_of(nq + x * rows, 8), rows), :]
+        attn = jnp.zeros((rows, LANES), jnp.float32)
+        for j in range(nx):
+            if j:
+                c_msg(r, j).wait_recv()
+            part = cin[r, j - 1] if j else cb[r, x]
+            share = jnp.where(lane < HD, mine_a[:, j:j + 1], mine_b[:, j:j + 1])
+            attn += share * part.astype(jnp.float32)
         pacc[...] += jnp.dot(
             attn.astype(jnp.bfloat16), w[pl.ds(r * LANES, LANES), :],
             preferred_element_type=jnp.float32,
         )
 
-    @pl.loop(pairs, total)
+    @pl.loop(before_q, total)
     def _(t):
         forward(t)
 
@@ -210,18 +242,14 @@
         def _(c):
             compute(c)
 
-        @pl.when(t >= total - pairs)
+        s, r = unit(t)
+
+        @pl.when(s == half)
         def _():
-            r = t - (total - pairs)
-            for j in range(1, nx):
-                st_msg(r, j).start()
+            spread(r)
 
     w_copy.wait()
     pacc[...] = jnp.zeros(pacc.shape, jnp.float32)
-
-    @pl.loop(0, pairs)
-    def _(r):
-        spread(r)
 
     @pl.loop(0, pairs)
     def _(r):
@@ -269,7 +297,7 @@
         out_features = out_weight.shape[1]
         nq = nx * rows
         dma = pltpu.SemaphoreType.DMA
-        any_space = pl.BlockSpec(memory_space=pl.ANY)
+        any_space = pl.BlockSpec(memory_space=pltpu.HBM)
         bf16, f32 = jnp.bfloat16, jnp.float32
         return pl.pallas_call(
             functools.partial(kernel, nz, nx),
@@ -287,6 +315,7 @@
                 pltpu.VMEM((pairs, nx, rows, LANES), bf16),
                 pltpu.VMEM((pairs, nx - 1, rows, LANES), bf16),
                 pltpu.VMEM((rows, out_features), f32),
+                pltpu.VMEM((2 * nq, LANES), f32),
                 pltpu.VMEM((rows // 2, out_features), bf16),
                 pltpu.VMEM((rows // 2, out_features), bf16),
                 dma((half, pairs, 2)), dma((half, pairs, 2)),
@@ -296,7 +325,7 @@
                 dma, dma, dma((pairs + 1, 2)),
             ],
             compiler_params=pltpu.CompilerParams(
-                collective_id=0, has_side_effects=True, vmem_limit_bytes=48 * 1024 * 1024
+                collective_id=0, has_side_effects=True, vmem_limit_bytes=67043328 - 256 * 1024
             ),
         )(query, key, value, out_weight)
 

time: 126 us -> 103 us (0.82)
  Pallas kernels: 121 us -> 101 us
  local copies, waits for them, and re-layouts: 4.87 us -> 1.61 us
    pallas_call x1, Pallas kernels: 121 us -> 101 us  [per_device(): pl.pallas_call(functools.partial(kernel, nz, nx), out_shape=jax.ShapeDtyp...]
    unnamed x9 -> x1, local copies, waits for them, and re-layouts: 4.87 us -> 1.61 us
where the time goes in v2:
time: 103 us
  Pallas kernels  101 us (98%)
  local copies, waits for them, and re-layouts  1.61 us (2%)
    pallas_call x1, Pallas kernels, per_device(): pl.pallas_call(functools.partial(kernel, nz, nx), out_shape=jax.ShapeDtyp...  101 us

profile of v2, /device:TPU:33, one launch (start us, length us, event | category | flops | bytes accessed | tf_op | source)
XLA Modules:
  0.0 102.9 jit_solution(10880252797426669892)
XLA Ops:
  0.0 101.3 %shard_map.46 = bf16[72,1280]{1,0:T(8,128)(2,1)} custom-call(bf16[144,640]{1,0:T(8,128)(2,1)} %q_hbm.1, bf16[144,640]{1,0:T(8,128)(2,1)} %k_hbm.1, bf16[144,640]{1,0:T(8,128)(2,1)} %v_hbm.1, bf16[640,1280]{1,0:T(8,128)(2,1)} %w_hbm.1), custom_call_target="tpu_custom_call" | custom-call | tf_op jit(solution)/shard_map/pallas_call | solution.py:302
  101.3 1.6 %copy.6 = bf16[72,1280]{1,0:T(8,128)(2,1)} copy(bf16[72,1280]{1,0:T(8,128)(2,1)} %shard_map.46) | data formatting | bytes 368640

commit v3 on v0

v3 whole, which is shorter than its diff:
```python
import functools
import math

import jax
import jax.numpy as jnp
from jax import lax
from jax.experimental import pallas as pl
from jax.experimental.pallas import tpu as pltpu
from jax.sharding import PartitionSpec as P

HD = 64
LANES = 128
GROUP = 4
MESH = pl.DeviceIdType.MESH


def up(n, m):
    return -(-n // m) * m


def kernel(
    nz, nx, near, q_hbm, k_hbm, v_hbm, w_hbm, out_ref,
    q_in, k_in, v_in, w, kvp, qp, kvb, qin, qrows, ml, acc, turned, ob, oin, attn, sbuf, rbuf,
    z_send, z_recv, q_send, q_recv, x_send, x_recv, d_send, d_recv, o_send, o_recv,
    p_send, p_recv, loc, own_sem,
):
    rows, features = q_hbm.shape
    heads = features // HD
    tiles = features // LANES
    half_rows = rows // 2
    half = nz // 2
    z = lax.axis_index("blk")
    x = lax.axis_index("node")
    p = lax.axis_index("pair")
    scale2 = (1.0 / math.sqrt(HD)) * math.log2(math.e)
    offsets = [0]
    for d in range(1, half):
        offsets += [d, -d]
    offsets.append(half)
    shared = [d for d in offsets if d % GROUP == 0]
    far = nz - near
    messages = near
    side = lax.div(z, half)
    in_side = z - side * half
    lead = lax.div(in_side, GROUP) * (GROUP + 1)
    head_own = lead + lax.rem(in_side, GROUP)
    head_shared = lead + GROUP
    split = up(far * rows, LANES)
    nq = ml.shape[1]

    def plane(d):
        return lax.rem(z + nz + d, nz)

    def node(j):
        return lax.rem(x + j, nx)

    barrier = pltpu.get_barrier_semaphore()
    for d in offsets[1:]:
        for c in range(2):
            pl.semaphore_signal(
                barrier, inc=1, device_id={"blk": plane(d), "pair": c}, device_id_type=MESH
            )
    for j in range(1, nx):
        pl.semaphore_signal(barrier, inc=1, device_id={"node": node(j)}, device_id_type=MESH)
    pl.semaphore_signal(barrier, inc=1, device_id={"pair": 1 - p}, device_id_type=MESH)

    loads = [
        pltpu.make_async_copy(src, dst, loc.at[i])
        for i, (src, dst) in enumerate(((q_hbm, q_in), (k_hbm, k_in), (v_hbm, v_in), (w_hbm, w)))
    ]
    for load in loads:
        load.start()

    low = lax.broadcasted_iota(jnp.int32, (rows, LANES), 1) < HD
    low_half = lax.broadcasted_iota(jnp.int32, (half_rows, LANES), 1) < HD

    def swap_sides(a):
        return pltpu.roll(a, HD, 1)

    loads[0].wait()
    for i in range(tiles):
        tile = q_in[:, i * LANES:(i + 1) * LANES].astype(jnp.float32)
        top, bottom = tile[:half_rows], tile[half_rows:]
        qp[2 * i] = jnp.where(low_half, top, swap_sides(bottom)).astype(jnp.bfloat16)
        qp[2 * i + 1] = jnp.where(low_half, swap_sides(top), bottom).astype(jnp.bfloat16)
    loads[1].wait()
    loads[2].wait()
    for i in range(tiles):
        k_tile = k_in[:, i * LANES:(i + 1) * LANES].astype(jnp.float32)
        v_tile = v_in[:, i * LANES:(i + 1) * LANES].astype(jnp.float32)
        kvp[2 * i] = jnp.where(low, k_tile, swap_sides(v_tile)).astype(jnp.bfloat16)
        kvp[2 * i + 1] = jnp.where(low, swap_sides(k_tile), v_tile).astype(jnp.bfloat16)
    ml[0:1, :] = jnp.full((1, nq), -1e30, jnp.float32)
    ml[1:2, :] = jnp.zeros((1, nq), jnp.float32)
    acc[...] = jnp.zeros(acc.shape, jnp.float32)
    qrows[...] = jnp.zeros(qrows.shape, jnp.bfloat16)

    def full_place(d):
        i = offsets.index(d)
        return (0, i) if i < near else (1, i - near)

    def shared_place(d):
        return 1, far + shared.index(d)

    def opposite(e):
        return half if e == half else -e

    def target_heads(zt):
        first = lax.div(zt - p * half, GROUP) * (GROUP + 1)
        return first + lax.rem(zt, GROUP), first + GROUP

    def kv_msg(e, kind):
        slot = offsets.index(opposite(e))
        zt = plane(e)
        return pltpu.make_async_remote_copy(
            src_ref=kvp.at[target_heads(zt)[kind]], dst_ref=kvb.at[0, slot, x],
            send_sem=z_send.at[slot, kind], recv_sem=z_recv.at[slot],
            device_id={"blk": zt, "pair": kind}, device_id_type=MESH,
        )

    def q_msg(e, kind):
        zt = plane(e)
        core, place = (full_place, shared_place)[kind](opposite(e))
        return pltpu.make_async_remote_copy(
            src_ref=qp.at[target_heads(zt)[kind]], dst_ref=qin.at[place],
            send_sem=q_send.at[offsets.index(e), kind], recv_sem=q_recv.at[place],
            device_id={"blk": zt, "pair": core}, device_id_type=MESH,
        )

    def mine(e):
        return lax.div(plane(e), half) == p

    def own_kv_local():
        return pltpu.make_async_copy(
            kvp.at[jnp.where(p == 0, head_own, head_shared)], kvb.at[0, 0, x], own_sem.at[0]
        )

    def own_kv_msg():
        return pltpu.make_async_remote_copy(
            src_ref=kvp.at[jnp.where(p == 0, head_shared, head_own)], dst_ref=kvb.at[0, 0, x],
            send_sem=z_send.at[0, 0], recv_sem=z_recv.at[0],
            device_id={"pair": 1 - p}, device_id_type=MESH,
        )

    def own_q_local():
        return pltpu.make_async_copy(
            qp.at[jnp.where(p == 0, head_own, head_shared)],
            qin.at[jnp.where(p == 0, 0, far)], own_sem.at[1],
        )

    def own_q_msg():
        there = jnp.where(p == 0, far, 0)
        return pltpu.make_async_remote_copy(
            src_ref=qp.at[jnp.where(p == 0, head_shared, head_own)], dst_ref=qin.at[there],
            send_sem=q_send.at[0, 0], recv_sem=q_recv.at[there],
            device_id={"pair": 1 - p}, device_id_type=MESH,
        )

    pl.semaphore_wait(barrier, 2 * (nz - 1) + nx)

    @pl.when(side == p)
    def _():
        own_q_local().start()
        own_kv_local().start()
        own_q_msg().start()
        own_kv_msg().start()

    for e in offsets[1:]:
        @pl.when(mine(e))
        def _():
            q_msg(e, 0).start()
            if e % GROUP == 0:
                q_msg(e, 1).start()
    for e in offsets[1:]:
        @pl.when(mine(e))
        def _():
            kv_msg(e, 0).start()
            kv_msg(e, 1).start()

    def x_msg(i, j):
        return pltpu.make_async_remote_copy(
            src_ref=kvb.at[0, i, x], dst_ref=kvb.at[0, i, x],
            send_sem=x_send.at[i, j - 1], recv_sem=x_recv.at[i, j - 1],
            device_id={"node": node(j)}, device_id_type=MESH,
        )

    def across(i, j):
        col = node(nx - j)
        return pltpu.make_async_remote_copy(
            src_ref=kvb.at[0, i, col], dst_ref=kvb.at[1, i, col],
            send_sem=d_send.at[i, j], recv_sem=d_recv.at[i, j],
            device_id={"pair": 1 - p}, device_id_type=MESH,
        )

    def arrive(i):
        @pl.when((i == 0) & (side == p))
        def _():
            own_kv_local().wait()

        @pl.when((i > 0) | (side != p))
        def _():
            pltpu.make_async_remote_copy(
                src_ref=kvb.at[0, i, x], dst_ref=kvb.at[0, i, x],
                send_sem=z_send.at[0, 0], recv_sem=z_recv.at[i],
                device_id={"pair": 1 - p}, device_id_type=MESH,
            ).wait_recv()

        for j in range(1, nx):
            x_msg(i, j).start()

        @pl.when(p == 0)
        def _():
            across(i, 0).start()

    def spread(i):
        for j in range(1, nx):
            col = node(nx - j)
            pltpu.make_async_remote_copy(
                src_ref=kvb.at[0, i, col], dst_ref=kvb.at[0, i, col],
                send_sem=x_send.at[i, j - 1], recv_sem=x_recv.at[i, j - 1],
                device_id={"node": node(j)}, device_id_type=MESH,
            ).wait_recv()

            @pl.when(p == 0)
            def _():
                across(i, j).start()

    width = 256
    spans = [(lo, min(lo + width, split), 1) for lo in range(0, split, width)]
    spans += [(hi, min(lo, nq), 0) for hi, lo in (
        [(split, up(split + 1, width))] + [(lo, lo + width) for lo in range(up(split + 1, width), nq, width)]
    ) if hi < nq]

    def compute(i):
        @pl.when(p == 1)
        def _():
            for j in range(nx):
                across(i, j).wait_recv()

        first = kvb[p, i].reshape(nx * rows, LANES)
        second = kvb[0, i].reshape(nx * rows, LANES)
        keys = (second, first)
        values = (second.T[HD:], first.T[HD:])

        def scored(span):
            lo, hi, kind = span
            sc = lax.dot_general(
                keys[kind], qrows[lo:hi, :], (((1,), (1,)), ((), ())),
                preferred_element_type=jnp.float32,
            )
            old = ml[0:1, lo:hi]
            return sc, old, jnp.maximum(old, jnp.max(sc, axis=0, keepdims=True))

        def weigh(span, sc, old, new):
            lo, hi, kind = span
            expo = jnp.exp2((sc - new) * scale2)
            factor = jnp.exp2((old - new) * scale2)
            total = ml[1:2, lo:hi] * factor + jnp.sum(expo, axis=0, keepdims=True)
            weighted = jnp.dot(
                values[kind], expo.astype(jnp.bfloat16), preferred_element_type=jnp.float32
            )
            return new, total, factor, weighted

        ready = scored(spans[0])
        results = []
        for n, span in enumerate(spans):
            following = scored(spans[n + 1]) if n + 1 < len(spans) else None
            results.append(weigh(span, *ready))
            ready = following
        for (lo, hi, _), (new, total, factor, weighted) in zip(spans, results):
            ml[0:1, lo:hi] = new
            ml[1:2, lo:hi] = total
            acc[:, lo:hi] = acc[:, lo:hi] * factor + weighted

    arrive(0)
    arrive(1)
    spread(0)

    def base(a):
        return pl.multiple_of(a * rows + jnp.where((p == 1) & (a >= far), split - far * rows, 0), 16)

    @pl.loop(0, messages)
    def _(a):
        own = (side == p) & (a == jnp.where(p == 0, 0, far))

        @pl.when(own)
        def _():
            own_q_local().wait()

        @pl.when(jnp.logical_not(own))
        def _():
            pltpu.make_async_remote_copy(
                src_ref=qin.at[a], dst_ref=qin.at[a], send_sem=q_send.at[0, 0],
                recv_sem=q_recv.at[a], device_id={"pair": 1 - p}, device_id_type=MESH,
            ).wait_recv()

        block = qin[a].astype(jnp.float32)
        both = jnp.concatenate(
            [jnp.where(low_half, block, 0.0), jnp.where(low_half, swap_sides(block), 0.0)], axis=0
        )
        qrows[pl.ds(base(a), rows), :] = both.astype(jnp.bfloat16)

    @pl.loop(0, nz)
    def _(i):
        @pl.when(i + 2 < nz)
        def _():
            arrive(i + 2)

        @pl.when(i + 1 < nz)
        def _():
            spread(i + 1)

        compute(i)

    def back(a):
        d = jnp.where(p == 0, offsets[a], (offsets[near:] + shared)[a])
        h = jnp.where((p == 1) & (a >= far), head_shared, head_own)
        return d, h

    def o_local(a):
        return pltpu.make_async_copy(ob.at[a], oin.at[back(a)[1]], own_sem.at[2])

    def o_msg(a):
        d, h = back(a)
        return pltpu.make_async_remote_copy(
            src_ref=ob.at[a], dst_ref=oin.at[h], send_sem=o_send.at[a], recv_sem=o_recv.at[h],
            device_id={"blk": plane(d), "pair": side}, device_id_type=MESH,
        )

    blank = jnp.zeros((LANES - HD, nq), jnp.float32)
    turned[...] = jnp.concatenate([acc[...] * (1.0 / ml[1:2, :]), blank], axis=0).T
    for a in range(messages):
        block = turned[pl.ds(base(a), rows), :]
        ob[a] = (block[:half_rows] + swap_sides(block[half_rows:])).astype(jnp.bfloat16)
        here = (back(a)[0] == 0) & (side == p)

        @pl.when(here)
        def _():
            o_local(a).start()

        @pl.when(jnp.logical_not(here))
        def _():
            o_msg(a).start()

    loads[3].wait()
    for i in range(tiles):
        for h in (2 * i, 2 * i + 1):
            g, n = divmod(h, GROUP + 1)
            zt = p * half + g * GROUP + (n if n < GROUP else lax.rem(z, GROUP))
            here = (zt == z) & (p == (0 if n < GROUP else 1))

            @pl.when(here)
            def _():
                pltpu.make_async_copy(ob.at[0], oin.at[h], own_sem.at[2]).wait()

            @pl.when(jnp.logical_not(here))
            def _():
                pltpu.make_async_remote_copy(
                    src_ref=oin.at[h], dst_ref=oin.at[h], send_sem=o_send.at[0],
                    recv_sem=o_recv.at[h], device_id={"pair": 1 - p}, device_id_type=MESH,
                ).wait_recv()

        even = oin[2 * i].astype(jnp.float32)
        odd = oin[2 * i + 1].astype(jnp.float32)
        cols = slice(i * LANES, (i + 1) * LANES)
        attn[0, :, cols] = jnp.where(low_half, even, swap_sides(odd)).astype(jnp.bfloat16)
        attn[1, :, cols] = jnp.where(low_half, swap_sides(even), odd).astype(jnp.bfloat16)

    sbuf[...] = jnp.dot(attn[1 - p], w[...], preferred_element_type=jnp.float32).astype(jnp.bfloat16)
    swap = pltpu.make_async_remote_copy(
        src_ref=sbuf, dst_ref=rbuf, send_sem=p_send, recv_sem=p_recv,
        device_id={"pair": 1 - p}, device_id_type=MESH,
    )
    swap.start()
    kept = jnp.dot(attn[p], w[...], preferred_element_type=jnp.float32)
    swap.wait_recv()
    out_ref[...] = (kept + rbuf[...].astype(jnp.float32)).astype(out_ref.dtype)
    swap.wait_send()

    @pl.when(side == p)
    def _():
        own_q_msg().wait_send()
        own_kv_msg().wait_send()

    for e in offsets[1:]:
        @pl.when(mine(e))
        def _():
            q_msg(e, 0).wait_send()
            if e % GROUP == 0:
                q_msg(e, 1).wait_send()
            kv_msg(e, 0).wait_send()
            kv_msg(e, 1).wait_send()

    @pl.loop(0, nz)
    def _(i):
        for j in range(1, nx):
            x_msg(i, j).wait_send()

        @pl.when(p == 0)
        def _():
            for j in range(nx):
                across(i, j).wait_send()

    for a in range(messages):
        @pl.when(jnp.logical_not((back(a)[0] == 0) & (side == p)))
        def _():
            o_msg(a).wait_send()


def solution(mesh):
    nz, nx = mesh.shape["blk"], mesh.shape["node"]

    def per_device(query, key, value, out_weight):
        rows, features = query.shape
        heads = features // HD
        assert nz % (2 * GROUP) == 0 and heads == nz // 2 // GROUP * (GROUP + 1)
        near = heads
        far = nz - near
        split = up(far * rows, LANES)
        nq = max(up(near * rows, LANES), split + up((nz // GROUP) * rows, LANES))
        out_features = out_weight.shape[1]
        dma = pltpu.SemaphoreType.DMA
        any_space = pl.BlockSpec(memory_space=pltpu.HBM)
        bf16, f32 = jnp.bfloat16, jnp.float32
        return pl.pallas_call(
            functools.partial(kernel, nz, nx, near),
            out_shape=jax.ShapeDtypeStruct((rows // 2, out_features), bf16),
            in_specs=[any_space] * 4,
            out_specs=pl.BlockSpec(memory_space=pltpu.VMEM),
            scratch_shapes=[
                pltpu.VMEM((rows, features), bf16),
                pltpu.VMEM((rows, features), bf16),
                pltpu.VMEM((rows, features), bf16),
                pltpu.VMEM((features, out_features), bf16),
                pltpu.VMEM((heads, rows, LANES), bf16),
                pltpu.VMEM((heads, rows // 2, LANES), bf16),
                pltpu.VMEM((2, nz, nx, rows, LANES), bf16),
                pltpu.VMEM((near, rows // 2, LANES), bf16),
                pltpu.VMEM((nq, LANES), bf16),
                pltpu.VMEM((2, nq), f32),
                pltpu.VMEM((HD, nq), f32),
                pltpu.VMEM((nq, LANES), f32),
                pltpu.VMEM((near, rows // 2, LANES), bf16),
                pltpu.VMEM((heads, rows // 2, LANES), bf16),
                pltpu.VMEM((2, rows // 2, features), bf16),
                pltpu.VMEM((rows // 2, out_features), bf16),
                pltpu.VMEM((rows // 2, out_features), bf16),
                dma((nz, 2)), dma((nz,)), dma((nz, 2)), dma((near,)),
                dma((nz, nx - 1)), dma((nz, nx - 1)), dma((nz, nx)), dma((nz, nx)),
                dma((near,)), dma((heads,)), dma, dma, dma((4,)), dma((3,)),
            ],
            compiler_params=pltpu.CompilerParams(
                collective_id=0, has_side_effects=True, vmem_limit_bytes=67043328 - 256 * 1024
            ),
        )(query, key, value, out_weight)

    tokens = P(("grp", "blk", "node"), "pair")
    return jax.shard_map(
        per_device,
        mesh=mesh,
        in_specs=(tokens, tokens, tokens, P("pair", None)),
        out_specs=P(("grp", "blk", "node", "pair"), None),
        check_vma=False,
    )
```

time: 284 us -> 110 us (0.39)
  Pallas kernels: 0 us -> 109 us
  waiting for transfers between devices: 87.2 us -> 0 us
  matrix products: 72.9 us -> 0 us
  other arithmetic: 36.7 us -> 0 us
  local copies, waits for them, and re-layouts: 37.3 us -> 1.61 us
  blocking collectives: 24.2 us -> 0 us
  between operations: 13.5 us -> 0.01 us
  starting transfers between devices: 11 us -> 0 us
    pallas_call x0 -> x1, Pallas kernels: none -> 109 us  [per_device(): pl.pallas_call(functools.partial(kernel, nz, nx, near), out_shape=jax.Sha...]
    all_gather x1 -> x0, waiting for transfers between devices: 79.6 us -> none  [in_one_piece(): lax.all_gather(both, axis, axis=dim, tiled=True)]
    dot_general x9 -> x0, matrix products: 72.9 us -> none  [the longest x4 38.5 us: update(): jnp.einsum('hqk,khd->qhd', expo.astype(jnp.bfloat16), value_block, prefer...]
    reduce_sum x7 -> x0, other arithmetic: 33.2 us -> none  [the longest x4 30.9 us: update(): total = total * factor + jnp.sum(expo, axis=2)]
    dynamic_slice x12 -> x0, local copies, waits for them, and re-layouts: 16.8 us -> none  [the longest x8 10.9 us: update(): lax.dynamic_slice_in_dim(values_piece, turn * size, size, 0)]
    all_to_all x1 -> x0, blocking collectives: 12.2 us -> none  [sent_and_summed(): tiles = lax.all_to_all(split_up(array, dim, length), axis, 0, 0, tiled=True)]
    all_gather x1 -> x0, blocking collectives: 12 us -> none  [per_device(): gathered = lax.all_gather(query, 'node', axis=0, tiled=True)]
    all_to_all x3 -> x0, starting transfers between devices: 11 us -> none  [the longest x1 3.99 us: per_device(): lax.all_to_all(peak_parts, 'node', split_axis=0, concat_axis=0, tiled=True)]
  transfers between devices with their start and end apart: 4 -> 0, of which waited for: 4 -> 0; matrix products, arithmetic and copies ran while one was open for 5% -> 0% of each run, Pallas kernels for 0% -> 0%
where the time goes in v3:
time: 110 us
  Pallas kernels  109 us (99%)
  local copies, waits for them, and re-layouts  1.61 us (1%)
    pallas_call x1, Pallas kernels, per_device(): pl.pallas_call(functools.partial(kernel, nz, nx, near), out_shape=jax.Sha...  109 us

profile of v3, /device:TPU:33, one launch (start us, length us, event | category | flops | bytes accessed | tf_op | source)
XLA Modules:
  0.0 110.3 jit_solution(3343903295122770552)
XLA Ops:
  0.0 108.7 %shard_map.46 = bf16[72,1280]{1,0:T(8,128)(2,1)} custom-call(bf16[144,640]{1,0:T(8,128)(2,1)} %q_hbm.1, bf16[144,640]{1,0:T(8,128)(2,1)} %k_hbm.1, bf16[144,640]{1,0:T(8,128)(2,1)} %v_hbm.1, bf16[640,1280]{1,0:T(8,128)(2,1)} %w_hbm.1), custom_call_target="tpu_custom_call" | custom-call | tf_op jit(solution)/shard_map/pallas_call | solution.py:425
  108.7 1.6 %copy.6 = bf16[72,1280]{1,0:T(8,128)(2,1)} copy(bf16[72,1280]{1,0:T(8,128)(2,1)} %shard_map.46) | data formatting | bytes 368640

commit v4 on v3

--- a/solution.py
+++ b/solution.py
@@ -171,26 +171,73 @@
             q_msg(e, 0).start()
             if e % GROUP == 0:
                 q_msg(e, 1).start()
-    for e in offsets[1:]:
-        @pl.when(mine(e))
-        def _():
-            kv_msg(e, 0).start()
-            kv_msg(e, 1).start()
-
-    def x_msg(i, j):
-        return pltpu.make_async_remote_copy(
-            src_ref=kvb.at[0, i, x], dst_ref=kvb.at[0, i, x],
-            send_sem=x_send.at[i, j - 1], recv_sem=x_recv.at[i, j - 1],
-            device_id={"node": node(j)}, device_id_type=MESH,
-        )
-
-    def across(i, j):
-        col = node(nx - j)
+    def kv_plane(n):
+        return plane(jnp.where(lax.rem(n, 2) == 1, lax.div(n + 1, 2), -lax.div(n, 2)))
+
+    def kv_out(n, kind):
+        odd = lax.rem(n, 2) == 1
+        slot = jnp.where(n == nz - 1, n, jnp.where(odd, n + 1, n - 1))
+        zt = kv_plane(n)
+        return pltpu.make_async_remote_copy(
+            src_ref=kvp.at[target_heads(zt)[kind]], dst_ref=kvb.at[0, slot, x],
+            send_sem=z_send.at[slot, kind], recv_sem=z_recv.at[slot],
+            device_id={"blk": zt, "pair": kind}, device_id_type=MESH,
+        )
+
+    def send_kv(n):
+        @pl.when(lax.div(kv_plane(n), half) == p)
+        def _():
+            kv_out(n, 0).start()
+            kv_out(n, 1).start()
+
+    window = 10
+
+    @pl.loop(1, window + 1)
+    def _(n):
+        send_kv(n)
+
+    ahead_hops = nx // 2
+    behind_hops = nx - 1 - ahead_hops
+    step = jnp.where(p == 0, 1, nx - 1)
+
+    def column(n):
+        return lax.rem(x + (n + nx) * (nx - step), nx)
+
+    def hop(i, n):
+        held = column(n - 1) if n > 0 else column(n + 1)
+        return pltpu.make_async_remote_copy(
+            src_ref=kvb.at[0, i, held], dst_ref=kvb.at[0, i, held],
+            send_sem=x_send.at[i, n + behind_hops], recv_sem=x_recv.at[i, n + behind_hops],
+            device_id={"node": column(-1 if n > 0 else 1)}, device_id_type=MESH,
+        )
+
+    def hop_arrived(i, n):
+        got = column(n)
+        pltpu.make_async_remote_copy(
+            src_ref=kvb.at[0, i, got], dst_ref=kvb.at[0, i, got],
+            send_sem=x_send.at[i, n + behind_hops], recv_sem=x_recv.at[i, n + behind_hops],
+            device_id={"node": column(-1)}, device_id_type=MESH,
+        ).wait_recv()
+
+    def across(i, n):
+        col = column(n)
         return pltpu.make_async_remote_copy(
             src_ref=kvb.at[0, i, col], dst_ref=kvb.at[1, i, col],
-            send_sem=d_send.at[i, j], recv_sem=d_recv.at[i, j],
+            send_sem=d_send.at[i, n + behind_hops], recv_sem=d_recv.at[i, n + behind_hops],
             device_id={"pair": 1 - p}, device_id_type=MESH,
         )
+
+    def across_arrived(i, n):
+        pltpu.make_async_remote_copy(
+            src_ref=kvb.at[1, i, 0], dst_ref=kvb.at[1, i, 0],
+            send_sem=d_send.at[i, n + behind_hops], recv_sem=d_recv.at[i, n + behind_hops],
+            device_id={"pair": 1 - p}, device_id_type=MESH,
+        ).wait_recv()
+
+    def hand_over(i, n):
+        @pl.when(p == 0)
+        def _():
+            across(i, n).start()
 
     def arrive(i):
         @pl.when((i == 0) & (side == p))
@@ -205,25 +252,21 @@
                 device_id={"pair": 1 - p}, device_id_type=MESH,
             ).wait_recv()
 
-        for j in range(1, nx):
-            x_msg(i, j).start()
-
-        @pl.when(p == 0)
-        def _():
-            across(i, 0).start()
-
-    def spread(i):
-        for j in range(1, nx):
-            col = node(nx - j)
-            pltpu.make_async_remote_copy(
-                src_ref=kvb.at[0, i, col], dst_ref=kvb.at[0, i, col],
-                send_sem=x_send.at[i, j - 1], recv_sem=x_recv.at[i, j - 1],
-                device_id={"node": node(j)}, device_id_type=MESH,
-            ).wait_recv()
-
-            @pl.when(p == 0)
-            def _():
-                across(i, j).start()
+        hop(i, 1).start()
+        if behind_hops:
+            hop(i, -1).start()
+        hand_over(i, 0)
+
+    def spread(i, n):
+        hop_arrived(i, n)
+        if n < ahead_hops:
+            hop(i, n + 1).start()
+        hand_over(i, n)
+        if n <= behind_hops:
+            hop_arrived(i, -n)
+            if n < behind_hops:
+                hop(i, -n - 1).start()
+            hand_over(i, -n)
 
     width = 256
     spans = [(lo, min(lo + width, split), 1) for lo in range(0, split, width)]
@@ -234,8 +277,8 @@
     def compute(i):
         @pl.when(p == 1)
         def _():
-            for j in range(nx):
-                across(i, j).wait_recv()
+            for n in range(-behind_hops, ahead_hops + 1):
+                across_arrived(i, n)
 
         first = kvb[p, i].reshape(nx * rows, LANES)
         second = kvb[0, i].reshape(nx * rows, LANES)
@@ -272,9 +315,9 @@
             ml[1:2, lo:hi] = total
             acc[:, lo:hi] = acc[:, lo:hi] * factor + weighted
 
-    arrive(0)
-    arrive(1)
-    spread(0)
+    gap = 2
+    for n in range(ahead_hops * gap + 1):
+        arrive(n)
 
     def base(a):
         return pl.multiple_of(a * rows + jnp.where((p == 1) & (a >= far), split - far * rows, 0), 16)
@@ -300,15 +343,24 @@
         )
         qrows[pl.ds(base(a), rows), :] = both.astype(jnp.bfloat16)
 
+    for m in range(1, ahead_hops + 1):
+        for n in range((ahead_hops - m) * gap + 1):
+            spread(n, m)
+
     @pl.loop(0, nz)
     def _(i):
-        @pl.when(i + 2 < nz)
-        def _():
-            arrive(i + 2)
-
-        @pl.when(i + 1 < nz)
-        def _():
-            spread(i + 1)
+        @pl.when(i + ahead_hops * gap + 1 < nz)
+        def _():
+            arrive(i + ahead_hops * gap + 1)
+
+        @pl.when(i + window + 1 < nz)
+        def _():
+            send_kv(i + window + 1)
+
+        for m in range(1, ahead_hops + 1):
+            @pl.when(i + (ahead_hops - m) * gap + 1 < nz)
+            def _():
+                spread(i + (ahead_hops - m) * gap + 1, m)
 
         compute(i)
 
@@ -393,13 +445,15 @@
 
     @pl.loop(0, nz)
     def _(i):
-        for j in range(1, nx):
-            x_msg(i, j).wait_send()
+        for n in range(1, ahead_hops + 1):
+            hop(i, n).wait_send()
+        for n in range(1, behind_hops + 1):
+            hop(i, -n).wait_send()
 
         @pl.when(p == 0)
         def _():
-            for j in range(nx):
-                across(i, j).wait_send()
+            for n in range(-behind_hops, ahead_hops + 1):
+                across(i, n).wait_send()
 
     for a in range(messages):
         @pl.when(jnp.logical_not((back(a)[0] == 0) & (side == p)))
@@ -446,7 +500,7 @@
                 pltpu.VMEM((rows // 2, out_features), bf16),
                 pltpu.VMEM((rows // 2, out_features), bf16),
                 dma((nz, 2)), dma((nz,)), dma((nz, 2)), dma((near,)),
-                dma((nz, nx - 1)), dma((nz, nx - 1)), dma((nz, nx)), dma((nz, nx)),
+                dma((nz, nx)), dma((nz, nx)), dma((nz, nx)), dma((nz, nx)),
                 dma((near,)), dma((heads,)), dma, dma, dma((4,)), dma((3,)),
             ],
             compiler_params=pltpu.CompilerParams(

time: 110 us -> 98.3 us (0.89)
  Pallas kernels: 109 us -> 96.6 us
    pallas_call x1, Pallas kernels: 109 us -> 96.6 us  [per_device(): pl.pallas_call(functools.partial(kernel, nz, nx, near), out_shape=jax.Sha...]
where the time goes in v4:
time: 98.3 us; the launch traced here: 98.2 us
  Pallas kernels  96.6 us (98%)
  local copies, waits for them, and re-layouts  1.61 us (2%)
    pallas_call x1, Pallas kernels, per_device(): pl.pallas_call(functools.partial(kernel, nz, nx, near), out_shape=jax.Sha...  96.6 us

profile of v4, /device:TPU:33, one launch (start us, length us, event | category | flops | bytes accessed | tf_op | source)
XLA Modules:
  0.0 98.2 jit_solution(2782034688585526168)
XLA Ops:
  0.0 96.6 %shard_map.46 = bf16[72,1280]{1,0:T(8,128)(2,1)} custom-call(bf16[144,640]{1,0:T(8,128)(2,1)} %q_hbm.1, bf16[144,640]{1,0:T(8,128)(2,1)} %k_hbm.1, bf16[144,640]{1,0:T(8,128)(2,1)} %v_hbm.1, bf16[640,1280]{1,0:T(8,128)(2,1)} %w_hbm.1), custom_call_target="tpu_custom_call" | custom-call | tf_op jit(solution)/shard_map/pallas_call | solution.py:479
  96.6 1.6 %copy.6 = bf16[72,1280]{1,0:T(8,128)(2,1)} copy(bf16[72,1280]{1,0:T(8,128)(2,1)} %shard_map.46) | data formatting | bytes 368640

commit v5 on v4

--- a/solution.py
+++ b/solution.py
@@ -347,22 +347,32 @@
         for n in range((ahead_hops - m) * gap + 1):
             spread(n, m)
 
-    @pl.loop(0, nz)
-    def _(i):
-        @pl.when(i + ahead_hops * gap + 1 < nz)
-        def _():
-            arrive(i + ahead_hops * gap + 1)
-
-        @pl.when(i + window + 1 < nz)
-        def _():
-            send_kv(i + window + 1)
+    lead_in = ahead_hops * gap + 1
+    tail = nz - lead_in + 2
+
+    def stage_end(n, m):
+        slack = (m - 1) * (gap - 1) + 1 if m <= ahead_hops else ahead_hops * (gap - 1)
+        late = jnp.clip(n - tail + 1, 0, slack)
+        return jnp.clip(n + 1 - gap * min(m, ahead_hops) - (m > ahead_hops) + late, 0, nz)
+
+    @pl.loop(lead_in, nz + ahead_hops + 1)
+    def _(n):
+        @pl.when(n < nz)
+        def _():
+            arrive(n)
+
+        @pl.when(n - lead_in + window + 1 < nz)
+        def _():
+            send_kv(n - lead_in + window + 1)
 
         for m in range(1, ahead_hops + 1):
-            @pl.when(i + (ahead_hops - m) * gap + 1 < nz)
-            def _():
-                spread(i + (ahead_hops - m) * gap + 1, m)
-
-        compute(i)
+            @pl.loop(stage_end(n - 1, m), stage_end(n, m))
+            def _(k):
+                spread(k, m)
+
+        @pl.loop(stage_end(n - 1, ahead_hops + 1), stage_end(n, ahead_hops + 1))
+        def _(k):
+            compute(k)
 
     def back(a):
         d = jnp.where(p == 0, offsets[a], (offsets[near:] + shared)[a])

time: 98.3 us -> 100 us (1.017)
  Pallas kernels: 96.6 us -> 98.6 us
    pallas_call x1, Pallas kernels: 96.6 us -> 98.6 us  [per_device(): pl.pallas_call(functools.partial(kernel, nz, nx, near), out_shape=jax.Sha...]
where the time goes in v5:
time: 100 us
  Pallas kernels  98.6 us (99%)
  local copies, waits for them, and re-layouts  1.61 us (2%)
    pallas_call x1, Pallas kernels, per_device(): pl.pallas_call(functools.partial(kernel, nz, nx, near), out_shape=jax.Sha...  98.6 us

profile of v5, /device:TPU:33, one launch (start us, length us, event | category | flops | bytes accessed | tf_op | source)
XLA Modules:
  0.0 100.2 jit_solution(7189023392525609970)
XLA Ops:
  0.0 98.6 %shard_map.46 = bf16[72,1280]{1,0:T(8,128)(2,1)} custom-call(bf16[144,640]{1,0:T(8,128)(2,1)} %q_hbm.1, bf16[144,640]{1,0:T(8,128)(2,1)} %k_hbm.1, bf16[144,640]{1,0:T(8,128)(2,1)} %v_hbm.1, bf16[640,1280]{1,0:T(8,128)(2,1)} %w_hbm.1), custom_call_target="tpu_custom_call" | custom-call | tf_op jit(solution)/shard_map/pallas_call | solution.py:489
  98.6 1.6 %copy.6 = bf16[72,1280]{1,0:T(8,128)(2,1)} copy(bf16[72,1280]{1,0:T(8,128)(2,1)} %shard_map.46) | data formatting | bytes 368640

commit v6 on v4

--- a/solution.py
+++ b/solution.py
@@ -190,7 +190,7 @@
             kv_out(n, 0).start()
             kv_out(n, 1).start()
 
-    window = 10
+    window = 12
 
     @pl.loop(1, window + 1)
     def _(n):
@@ -315,7 +315,7 @@
             ml[1:2, lo:hi] = total
             acc[:, lo:hi] = acc[:, lo:hi] * factor + weighted
 
-    gap = 2
+    gap = 3
     for n in range(ahead_hops * gap + 1):
         arrive(n)
 

time: 98.3 us -> 101 us (1.027)
  Pallas kernels: 96.6 us -> 98.9 us
    pallas_call x1, Pallas kernels: 96.6 us -> 98.9 us  [per_device(): pl.pallas_call(functools.partial(kernel, nz, nx, near), out_shape=jax.Sha...]
where the time goes in v6:
time: 101 us
  Pallas kernels  98.9 us (98%)
  local copies, waits for them, and re-layouts  1.61 us (2%)
    pallas_call x1, Pallas kernels, per_device(): pl.pallas_call(functools.partial(kernel, nz, nx, near), out_shape=jax.Sha...  98.9 us

profile of v6, /device:TPU:33, one launch (start us, length us, event | category | flops | bytes accessed | tf_op | source)
XLA Modules:
  0.0 100.6 jit_solution(10756135207772125003)
XLA Ops:
  0.0 98.9 %shard_map.46 = bf16[72,1280]{1,0:T(8,128)(2,1)} custom-call(bf16[144,640]{1,0:T(8,128)(2,1)} %q_hbm.1, bf16[144,640]{1,0:T(8,128)(2,1)} %k_hbm.1, bf16[144,640]{1,0:T(8,128)(2,1)} %v_hbm.1, bf16[640,1280]{1,0:T(8,128)(2,1)} %w_hbm.1), custom_call_target="tpu_custom_call" | custom-call | tf_op jit(solution)/shard_map/pallas_call | solution.py:479
  99.0 1.6 %copy.6 = bf16[72,1280]{1,0:T(8,128)(2,1)} copy(bf16[72,1280]{1,0:T(8,128)(2,1)} %shard_map.46) | data formatting | bytes 368640
